TPU v7x, 32 devices: a whole 2x2x4 slice. The times are simulated.
32 devices in a mesh: tok: 4 (over z), out: 4 (over x, core), grp: 2 (over y).
Axes of the slice: x: 2, y: 2, z: 4, core: 2. Of those that a mesh axis runs over, the one named last changes fastest.
Arguments:
- activations: bfloat16 [1024, 2, 2048], P(('tok', 'grp'), None, 'out'), may hold values from -16 to 16
- out_grads: bfloat16 [1024, 2, 2048], P(('tok', 'grp'), None, 'out'), may hold values from -16 to 16
- weight: bfloat16 [2, 2048, 4096], P(None, 'out'), may hold values from -0.09375 to 0.09375
Outputs:
- update: bfloat16 [4096, 2, 2048], P(('tok', 'grp'), None, 'out')
- input_grad: bfloat16 [1024, 2, 2048], P(('tok', 'grp'), None, 'out')
All inputs are finite; a program needn't handle non-finite values.
Results may differ from a plain program's by a relative error of at most 0.0092.
Values may be sent and summed in bfloat16 or wider, within the bound.
A program may use at most 64 MiB of HBM per device.

v0:
```python
import math
import jax
import jax.numpy as jnp
from jax import lax
from jax.sharding import PartitionSpec as P

POWER = 3
DAMPING = 0.1
HIGH = lax.Precision.HIGHEST


def spread(piece):
    return lax.all_gather(piece, "out", axis=2, tiled=True)


def token_sums(maker, rows):
    return lax.psum_scatter(
        maker(jnp.int32(0), rows * lax.axis_size(("tok", "grp"))),
        ("tok", "grp"),
        scatter_dimension=0,
        tiled=True,
    )


def shared_rows(piece):
    return lax.all_gather(piece, ("tok", "grp"), axis=0, tiled=True)


def shared_total(vector):
    return lax.psum(vector, ("tok", "out", "grp"))


def diagonal_mask(rows, width, row_start, col_start):
    row_ids = row_start + lax.broadcasted_iota(jnp.int32, (rows, 1, width), 0)
    col_ids = col_start + lax.broadcasted_iota(jnp.int32, (rows, 1, width), 2)
    return jnp.where(row_ids == col_ids, 1.0, 0.0).astype(jnp.float32)


def multiply(left, right, gather_columns):
    row_band = spread(left)
    column_band = gather_columns(right)
    return jnp.einsum("rkj,jkc->rkc", row_band, column_band, preferred_element_type=jnp.float32)


def inverse_roots(tile, row_start, col_start, gather_columns, total):
    rows, count, width = tile.shape
    block = width * lax.axis_size("out")
    mask = diagonal_mask(rows, width, row_start, col_start)
    vector = jnp.ones((count, block), jnp.float32)
    image = vector
    for step in range(POWER):
        columns = lax.dynamic_slice_in_dim(vector, col_start, width, 1)
        part = jnp.einsum("rkc,kc->kr", tile, columns, precision=HIGH)
        placed = lax.dynamic_update_slice_in_dim(
            jnp.zeros((count, block), jnp.float32), part, row_start, 1
        )
        image = total(placed)
        if step + 1 < POWER:
            vector = image / jnp.sqrt(jnp.sum(image * image, axis=1, keepdims=True))
    scale = jnp.sum(vector * image, axis=1) / jnp.sum(vector * vector, axis=1)
    start = tile / scale[None, :, None]
    start_low = start.astype(jnp.bfloat16)
    first_low = ((3.0 * mask - start) / 2.0).astype(jnp.bfloat16)
    square_low = multiply(first_low, first_low, gather_columns).astype(jnp.bfloat16)
    moved = multiply(square_low, start_low, gather_columns)
    second_low = ((3.0 * mask - moved) / 2.0).astype(jnp.bfloat16)
    roots = multiply(first_low, second_low, gather_columns) / jnp.sqrt(scale)[None, :, None]
    return roots.astype(jnp.bfloat16)


def local(activations, out_grads, weight):
    tok_dev, blocks, width = activations.shape
    block = width * lax.axis_size("out")
    token_count = tok_dev * lax.axis_size("tok") * lax.axis_size("grp")
    col_start = lax.axis_index("out") * width
    local_sides = jnp.concatenate([activations, out_grads], axis=1)
    whole_sides = spread(local_sides)
    grads_whole = whole_sides[:, blocks:, :]
    weight_rows = weight.reshape(blocks, width, blocks, block)
    input_grad = jnp.einsum(
        "tjq,bcjq->tbc", grads_whole, weight_rows, preferred_element_type=jnp.float32
    ).astype(jnp.bfloat16)
    rows = block // (lax.axis_size("tok") * lax.axis_size("grp"))
    row_start = lax.axis_index(("tok", "grp")) * rows

    def shared_terms(start, span):
        return jnp.einsum(
            "tkr,tkc->rkc", whole_sides, local_sides, preferred_element_type=jnp.float32
        )

    sums = token_sums(shared_terms, rows)
    tile = sums / token_count + DAMPING * diagonal_mask(rows, width, row_start, col_start)
    roots = inverse_roots(tile, row_start, col_start, shared_rows, shared_total)
    bands = shared_rows(roots)
    whitened = jnp.einsum(
        "tkj,jkc->tkc", whole_sides, bands, preferred_element_type=jnp.float32
    ).astype(jnp.bfloat16)
    acts_whole = spread(whitened[:, :blocks, :]).reshape(tok_dev, blocks * block)
    grads_low = whitened[:, blocks:, :]
    owned_acts = lax.all_to_all(acts_whole, ("tok", "grp"), split_axis=1, concat_axis=0, tiled=True)
    update = jnp.einsum(
        "ta,tbc->abc",
        owned_acts,
        lax.all_gather(grads_low, ("tok", "grp"), axis=0, tiled=True),
        preferred_element_type=jnp.float32,
    )
    update = (update / math.sqrt(token_count)).astype(jnp.bfloat16)
    return (update, input_grad)


def solution(mesh):
    in_specs = (
        P(("tok", "grp"), None, "out"),
        P(("tok", "grp"), None, "out"),
        P(None, "out", None),
    )
    out_specs = (P(("tok", "grp"), None, "out"), P(("tok", "grp"), None, "out"))
    return jax.shard_map(local, mesh=mesh, in_specs=in_specs, out_specs=out_specs, check_vma=False)
```

profile of v0, /device:TPU:0, one launch (start us, length us, event | category | flops | bytes accessed | tf_op | source)
XLA Modules:
  0.0 1136.9 jit_solution(8817919165431428209)
XLA Ops:
  10.0 25.4 %all-gather.10.cloned.1.call-done = bf16[128,4,2048]{2,0,1:T(8,128)(2,1)} async-done(((bf16[128,4,512]{2,0,1:T(8,128)(2,1)}), bf16[128,4,2048]{2,0,1:T(8,128)(2,1)}) %all-gather.10.cloned.1.call-update) | async-done | bytes 2097168 | tf_op jit(solution)/shard_map/all_gather | solution.py:13
  35.4 9.9 convolution_bitcast_fusion
  45.6 280.1 %reduce-scatter.2.cloned.1.call-done = f32[256,4,512]{0,2,1:T(8,128)} async-done(((f32[2048,4,512]{0,2,1:T(8,128)}), f32[256,4,512]{0,2,1:T(8,128)}) %reduce-scatter.2.cloned.1.call-update) | async-done | bytes 2097168 | tf_op jit(solution)/shard_map/reduce_scatter | solution.py:17
  325.7 3.0 fusion.10
  328.7 39.4 %psum.21 = f32[4,2048]{1,0:T(4,128)S(1)} all-reduce(f32[4,2048]{1,0:T(4,128)S(1)} %bitcast_dynamic-update-slice_fusion.2), channel_id=1, replica_groups=mesh['tok'=4,'out'=4,'grp'=2] {'tok','out','grp'}, use_global_device_ids=true, to_apply=%region_1.2 | all-reduce | flops 8192 | bytes 65536 | tf_op jit(solution)/shard_map/psum | solution.py:30
  369.8 39.9 %psum.22 = f32[4,2048]{1,0:T(4,128)S(1)} all-reduce(f32[4,2048]{1,0:T(4,128)S(1)} %bitcast_dynamic-update-slice_fusion.1), channel_id=1, replica_groups=mesh['tok'=4,'out'=4,'grp'=2] {'tok','out','grp'}, use_global_device_ids=true, to_apply=%region_3.4 | all-reduce | flops 8192 | bytes 65536 | tf_op jit(solution)/shard_map/psum | solution.py:30
  411.3 40.3 %psum.23 = f32[4,2048]{1,0:T(4,128)S(1)} all-reduce(f32[4,2048]{1,0:T(4,128)S(1)} %bitcast_dynamic-update-slice_fusion), channel_id=1, replica_groups=mesh['tok'=4,'out'=4,'grp'=2] {'tok','out','grp'}, use_global_device_ids=true, to_apply=%region_5.6 | all-reduce | flops 8192 | bytes 65536 | tf_op jit(solution)/shard_map/psum | solution.py:30
  454.8 33.2 %all-gather.16.cloned.1.call-done = bf16[256,4,2048]{0,2,1:T(8,128)(2,1)} async-done(((bf16[256,4,512]{0,2,1:T(8,128)(2,1)}), bf16[256,4,2048]{0,2,1:T(8,128)(2,1)}) %all-gather.16.cloned.1.call-update) | async-done | bytes 4194320 | tf_op jit(solution)/shard_map/all_gather | solution.py:13
  488.0 127.4 %all-gather.14.cloned.1.call-done = bf16[2048,4,512]{0,2,1:T(8,128)(2,1)} async-done(((bf16[256,4,512]{0,2,1:T(8,128)(2,1)}), bf16[2048,4,512]{0,2,1:T(8,128)(2,1)}) %all-gather.14.cloned.1.call-update) | async-done | bytes 8388624 | tf_op jit(solution)/shard_map/all_gather | solution.py:26
  615.5 7.9 fusion.5
  623.6 116.9 %all-gather.12.cloned.1.call-done = bf16[2048,4,512]{0,2,1:T(8,128)(2,1)} async-done(((bf16[256,4,512]{0,2,1:T(8,128)(2,1)}), bf16[2048,4,512]{0,2,1:T(8,128)(2,1)}) %all-gather.12.cloned.1.call-update) | async-done | bytes 8388624 | tf_op jit(solution)/shard_map/all_gather | solution.py:26
  740.5 34.7 %all-gather.18.cloned.1.call-done = bf16[256,4,2048]{0,2,1:T(8,128)(2,1)} async-done(((bf16[256,4,512]{0,2,1:T(8,128)(2,1)}), bf16[256,4,2048]{0,2,1:T(8,128)(2,1)}) %all-gather.18.cloned.1.call-update) | async-done | bytes 4194320 | tf_op jit(solution)/shard_map/all_gather | solution.py:13
  775.2 7.9 fusion.4
  783.1 125.0 %all-gather.20.cloned.1.call-done = bf16[2048,4,512]{0,2,1:T(8,128)(2,1)} async-done(((bf16[256,4,512]{0,2,1:T(8,128)(2,1)}), bf16[2048,4,512]{0,2,1:T(8,128)(2,1)}) %all-gather.20.cloned.1.call-update) | async-done | bytes 8388624 | tf_op jit(solution)/shard_map/all_gather | solution.py:26
  908.2 8.0 fusion.6
  916.3 123.2 %all-gather.22.cloned.1.call-done = bf16[2048,4,512]{0,2,1:T(8,128)(2,1)} async-done(((bf16[256,4,512]{0,2,1:T(8,128)(2,1)}), bf16[2048,4,512]{0,2,1:T(8,128)(2,1)}) %all-gather.22.cloned.1.call-update) | async-done | bytes 8388624 | tf_op jit(solution)/shard_map/all_gather | solution.py:26
  1039.5 5.7 fusion.11
  1046.6 14.4 %all-gather.24.cloned.1.call-done = bf16[128,2,2048]{0,2,1:T(8,128)(2,1)} async-done(((bf16[128,2,512]{0,2,1:T(8,128)(2,1)}), bf16[128,2,2048]{0,2,1:T(8,128)(2,1)}) %all-gather.24.cloned.1.call-update) | async-done | bytes 1048592 | tf_op jit(solution)/shard_map/all_gather | solution.py:13
  1061.1 5.5 all-to-all-start
  1066.6 6.3 fusion.15
  1073.8 27.3 %all-to-all-done = bf16[128,8,512]{0,2,1:T(8,128)(2,1)S(1)} async-done(((bf16[128,8,512]{0,2,1:T(8,128)(2,1)}), bf16[128,8,512]{0,2,1:T(8,128)(2,1)S(1)}, u32[]{:S(2)}, u32[]{:S(2)}) %all-to-all-start) | async-done | bytes 1048608 | tf_op jit(solution)/shard_map/all_to_all | solution.py:100
  1102.4 22.7 %all-gather.26.cloned.1.call-done = bf16[1024,2,512]{0,2,1:T(8,128)(2,1)} async-done(((bf16[128,2,512]{0,2,1:T(8,128)(2,1)}), bf16[1024,2,512]{0,2,1:T(8,128)(2,1)}) %all-gather.26.cloned.1.call-update) | async-done | bytes 2097168 | tf_op jit(solution)/shard_map/all_gather | solution.py:104
  1125.1 2.9 multiply_convert_fusion
  1128.0 2.0 copy.19
  (53 shorter events, 13.3 us)
Async XLA Ops:
  7.2 28.3 %all-gather.10.cloned.1.call-start = ((), (), s32[]{:S(2)}) async-start(), calls=%async_computation.2 | async-start | bytes 2621440 | tf_op jit(solution)/shard_map/all_gather | solution.py:13
  9.2 0.8 copy-start.1
  10.0 315.7 %reduce-scatter.2.cloned.1.call-start = ((), (), s32[]{:S(2)}) async-start(), calls=%async_computation.3 | async-start | bytes 18874368 | tf_op jit(solution)/shard_map/reduce_scatter | solution.py:17
  45.3 442.7 %all-gather.16.cloned.1.call-start = ((), (), s32[]{:S(2)}) async-start(), calls=%async_computation.6 | async-start | bytes 5242880 | tf_op jit(solution)/shard_map/all_gather | solution.py:13
  325.7 42.7 %copy-start = (f32[256,4,512]{0,2,1:T(8,128)S(1)}, f32[256,4,512]{0,2,1:T(8,128)}, u32[]{:S(2)}) copy-start(f32[256,4,512]{0,2,1:T(8,128)} %reduce-scatter.2.cloned.1.call-done) | copy-start | bytes 6291460
  453.6 161.9 %all-gather.14.cloned.1.call-start = ((), (), s32[]{:S(2)}) async-start(), calls=%async_computation.5 | async-start | bytes 9437184 | tf_op jit(solution)/shard_map/all_gather | solution.py:26
  454.2 286.3 %all-gather.12.cloned.1.call-start = ((), (), s32[]{:S(2)}) async-start(), calls=%async_computation.4 | async-start | bytes 9437184 | tf_op jit(solution)/shard_map/all_gather | solution.py:26
  454.8 320.4 %all-gather.18.cloned.1.call-start = ((), (), s32[]{:S(2)}) async-start(), calls=%async_computation.7 | async-start | bytes 5242880 | tf_op jit(solution)/shard_map/all_gather | solution.py:13
  623.4 284.8 %all-gather.20.cloned.1.call-start = ((), (), s32[]{:S(2)}) async-start(), calls=%async_computation.8 | async-start | bytes 9437184 | tf_op jit(solution)/shard_map/all_gather | solution.py:26
  783.1 256.4 %all-gather.22.cloned.1.call-start = ((), (), s32[]{:S(2)}) async-start(), calls=%async_computation.9 | async-start | bytes 9437184 | tf_op jit(solution)/shard_map/all_gather | solution.py:26
  908.2 131.3 %copy-start.2 = (bf16[128,4,2048]{2,0,1:T(8,128)(2,1)S(1)}, bf16[128,4,2048]{2,0,1:T(8,128)(2,1)}, u32[]{:S(2)}) copy-start(bf16[128,4,2048]{2,0,1:T(8,128)(2,1)} %all-gather.10.cloned.1.call-done) | copy-start | bytes 6291460
  916.2 144.9 %all-gather.24.cloned.1.call-start = ((), (), s32[]{:S(2)}) async-start(), calls=%async_computation.10 | async-start | bytes 1310720 | tf_op jit(solution)/shard_map/all_gather | solution.py:13
  1046.1 79.0 %all-gather.26.cloned.1.call-start = ((), (), s32[]{:S(2)}) async-start(), calls=%async_computation.11 | async-start | bytes 2359296 | tf_op jit(solution)/shard_map/all_gather | solution.py:104
  1061.1 40.1 %all-to-all-start = ((bf16[128,8,512]{0,2,1:T(8,128)(2,1)}), bf16[128,8,512]{0,2,1:T(8,128)(2,1)S(1)}, u32[]{:S(2)}, u32[]{:S(2)}) async-start(bf16[128,8,512]{0,2,1:T(8,128)(2,1)} %bitcast.57), calls=%async_computation.1 | async-start | bytes 2097152 | tf_op jit(solution)/shard_map/all_to_all | solution.py:100
Sparse Core Ops, SparseCore 0:
  10.1 25.2 all-gather.9
  45.5 280.1 reduce-scatter.1
  453.7 34.2 all-gather.15
  490.5 124.9 all-gather.13
  617.4 123.1 all-gather.11
  742.5 32.6 all-gather.17
  783.2 124.9 all-gather.19
  916.3 123.1 all-gather.21
  1046.2 14.8 all-gather.23
  1063.5 61.5 all-gather.25
where the time goes:
time: 1140 us
  waiting for transfers between devices  932 us (82%)
  blocking collectives  120 us (11%)
  matrix products  54.2 us (5%)
  between operations  14.3 us (1%)
    all_gather x4, waiting for transfers between devices, shared_rows(): return lax.all_gather(piece, ('tok', 'grp'), axis=0, tiled=True)  493 us
    reduce_scatter x1, waiting for transfers between devices, token_sums(): lax.psum_scatter(maker(jnp.int32(0), rows * lax.axis_size(('tok', 'grp'))...  280 us
    psum x3, blocking collectives, shared_total(): return lax.psum(vector, ('tok', 'out', 'grp'))  120 us
    all_gather x4, waiting for transfers between devices, spread(): return lax.all_gather(piece, 'out', axis=2, tiled=True)  108 us
    all_to_all x1, waiting for transfers between devices, local(): lax.all_to_all(acts_whole, ('tok', 'grp'), split_axis=1, concat_axis=0, t...  27.3 us
    dot_general x3, matrix products, multiply(): jnp.einsum('rkj,jkc->rkc', row_band, column_band, preferred_element_type=...  23.8 us
  transfers between devices with their start and end apart: 11, of which 11 were waited for; matrix products, arithmetic and copies ran while one was open for 1% of the time, Pallas kernels for 0%

commit v1 on v0

--- a/solution.py
+++ b/solution.py
@@ -1,3 +1,4 @@
+import functools
 import math
 import jax
 import jax.numpy as jnp
@@ -7,6 +8,13 @@
 POWER = 3
 DAMPING = 0.1
 HIGH = lax.Precision.HIGHEST
+
+
+def keep_up_the_groups(x0, axis_tag):
+    return jnp.sum(lax.all_gather(x0, axis_name=axis_tag), axis=0)
+
+
+settle_spots = functools.partial(keep_up_the_groups, axis_tag=("tok", "out", "grp"))
 
 
 def spread(piece):
@@ -27,7 +35,7 @@
 
 
 def shared_total(vector):
-    return lax.psum(vector, ("tok", "out", "grp"))
+    return settle_spots(vector)
 
 
 def diagonal_mask(rows, width, row_start, col_start):

time: 1140 us -> 1180 us (1.035)
  waiting for transfers between devices: 932 us -> 1090 us
  blocking collectives: 120 us -> 0 us
    all_gather x0 -> x3, waiting for transfers between devices: none -> 159 us  [keep_up_the_groups(): return jnp.sum(lax.all_gather(x0, axis_name=axis_tag), axis=0)]
    psum x3 -> x0, blocking collectives: 120 us -> none  [shared_total(): return lax.psum(vector, ('tok', 'out', 'grp'))]
  transfers between devices with their start and end apart: 11 -> 14, of which waited for: 11 -> 14; matrix products, arithmetic and copies ran while one was open for 1% -> 1% of each run, Pallas kernels for 0% -> 0%
where the time goes in v1:
time: 1180 us
  waiting for transfers between devices  1090 us (92%)
  matrix products  54.2 us (5%)
  between operations  14 us (1%)
    all_gather x4, waiting for transfers between devices, shared_rows(): return lax.all_gather(piece, ('tok', 'grp'), axis=0, tiled=True)  493 us
    reduce_scatter x1, waiting for transfers between devices, token_sums(): lax.psum_scatter(maker(jnp.int32(0), rows * lax.axis_size(('tok', 'grp'))...  280 us
    all_gather x3, waiting for transfers between devices, keep_up_the_groups(): return jnp.sum(lax.all_gather(x0, axis_name=axis_tag), axis=0)  159 us
    all_gather x4, waiting for transfers between devices, spread(): return lax.all_gather(piece, 'out', axis=2, tiled=True)  107 us
    all_to_all x1, waiting for transfers between devices, local(): lax.all_to_all(acts_whole, ('tok', 'grp'), split_axis=1, concat_axis=0, t...  27.3 us
    dot_general x3, matrix products, multiply(): jnp.einsum('rkj,jkc->rkc', row_band, column_band, preferred_element_type=...  23.8 us
  transfers between devices with their start and end apart: 14, of which 14 were waited for; matrix products, arithmetic and copies ran while one was open for 1% of the time, Pallas kernels for 0%

profile of v1, /device:TPU:0, one launch (start us, length us, event | category | flops | bytes accessed | tf_op | source)
XLA Modules:
  0.0 1181.4 jit_solution(15112005716104359299)
XLA Ops:
  10.0 25.4 %all-gather.13.cloned.1.call-done = bf16[128,4,2048]{2,0,1:T(8,128)(2,1)} async-done(((bf16[128,4,512]{2,0,1:T(8,128)(2,1)}), bf16[128,4,2048]{2,0,1:T(8,128)(2,1)}) %all-gather.13.cloned.1.call-update) | async-done | bytes 2097168 | tf_op jit(solution)/shard_map/all_gather | solution.py:21
  35.4 9.9 convolution_bitcast_fusion
  45.5 280.1 %reduce-scatter.2.cloned.1.call-done = f32[256,4,512]{0,2,1:T(8,128)} async-done(((f32[2048,4,512]{0,2,1:T(8,128)}), f32[256,4,512]{0,2,1:T(8,128)}) %reduce-scatter.2.cloned.1.call-update) | async-done | bytes 2097168 | tf_op jit(solution)/shard_map/reduce_scatter | solution.py:25
  325.7 3.0 fusion.10
  329.4 53.0 %all-gather.15.cloned.1.call-done = f32[32,4,2048]{2,1,0:T(4,128)} async-done(((f32[1,4,2048]{2,1,0:T(4,128)}), f32[32,4,2048]{2,1,0:T(4,128)}) %all-gather.15.cloned.1.call-update) | async-done | bytes 1048592 | tf_op jit(solution)/shard_map/all_gather | solution.py:14
  386.0 52.8 %all-gather.17.cloned.1.call-done = f32[32,4,2048]{2,1,0:T(4,128)} async-done(((f32[1,4,2048]{2,1,0:T(4,128)}), f32[32,4,2048]{2,1,0:T(4,128)}) %all-gather.17.cloned.1.call-update) | async-done | bytes 1048592 | tf_op jit(solution)/shard_map/all_gather | solution.py:14
  442.5 52.8 %all-gather.19.cloned.1.call-done = f32[32,4,2048]{2,1,0:T(4,128)} async-done(((f32[1,4,2048]{2,1,0:T(4,128)}), f32[32,4,2048]{2,1,0:T(4,128)}) %all-gather.19.cloned.1.call-update) | async-done | bytes 1048592 | tf_op jit(solution)/shard_map/all_gather | solution.py:14
  500.3 32.0 %all-gather.25.cloned.1.call-done = bf16[256,4,2048]{0,2,1:T(8,128)(2,1)} async-done(((bf16[256,4,512]{0,2,1:T(8,128)(2,1)}), bf16[256,4,2048]{0,2,1:T(8,128)(2,1)}) %all-gather.25.cloned.1.call-update) | async-done | bytes 4194320 | tf_op jit(solution)/shard_map/all_gather | solution.py:21
  532.4 127.6 %all-gather.23.cloned.1.call-done = bf16[2048,4,512]{0,2,1:T(8,128)(2,1)} async-done(((bf16[256,4,512]{0,2,1:T(8,128)(2,1)}), bf16[2048,4,512]{0,2,1:T(8,128)(2,1)}) %all-gather.23.cloned.1.call-update) | async-done | bytes 8388624 | tf_op jit(solution)/shard_map/all_gather | solution.py:34
  660.0 7.9 fusion.5
  668.1 117.1 %all-gather.21.cloned.1.call-done = bf16[2048,4,512]{0,2,1:T(8,128)(2,1)} async-done(((bf16[256,4,512]{0,2,1:T(8,128)(2,1)}), bf16[2048,4,512]{0,2,1:T(8,128)(2,1)}) %all-gather.21.cloned.1.call-update) | async-done | bytes 8388624 | tf_op jit(solution)/shard_map/all_gather | solution.py:34
  785.2 34.8 %all-gather.27.cloned.1.call-done = bf16[256,4,2048]{0,2,1:T(8,128)(2,1)} async-done(((bf16[256,4,512]{0,2,1:T(8,128)(2,1)}), bf16[256,4,2048]{0,2,1:T(8,128)(2,1)}) %all-gather.27.cloned.1.call-update) | async-done | bytes 4194320 | tf_op jit(solution)/shard_map/all_gather | solution.py:21
  820.0 7.9 fusion.4
  827.9 125.0 %all-gather.29.cloned.1.call-done = bf16[2048,4,512]{0,2,1:T(8,128)(2,1)} async-done(((bf16[256,4,512]{0,2,1:T(8,128)(2,1)}), bf16[2048,4,512]{0,2,1:T(8,128)(2,1)}) %all-gather.29.cloned.1.call-update) | async-done | bytes 8388624 | tf_op jit(solution)/shard_map/all_gather | solution.py:34
  953.0 8.0 fusion.6
  961.1 123.2 %all-gather.31.cloned.1.call-done = bf16[2048,4,512]{0,2,1:T(8,128)(2,1)} async-done(((bf16[256,4,512]{0,2,1:T(8,128)(2,1)}), bf16[2048,4,512]{0,2,1:T(8,128)(2,1)}) %all-gather.31.cloned.1.call-update) | async-done | bytes 8388624 | tf_op jit(solution)/shard_map/all_gather | solution.py:34
  1084.3 5.7 fusion.11
  1091.6 14.3 %all-gather.33.cloned.1.call-done = bf16[128,2,2048]{0,2,1:T(8,128)(2,1)} async-done(((bf16[128,2,512]{0,2,1:T(8,128)(2,1)}), bf16[128,2,2048]{0,2,1:T(8,128)(2,1)}) %all-gather.33.cloned.1.call-update) | async-done | bytes 1048592 | tf_op jit(solution)/shard_map/all_gather | solution.py:21
  1105.9 5.5 all-to-all-start
  1111.4 6.3 fusion.15
  1118.6 27.3 %all-to-all-done = bf16[128,8,512]{0,2,1:T(8,128)(2,1)S(1)} async-done(((bf16[128,8,512]{0,2,1:T(8,128)(2,1)}), bf16[128,8,512]{0,2,1:T(8,128)(2,1)S(1)}, u32[]{:S(2)}, u32[]{:S(2)}) %all-to-all-start) | async-done | bytes 1048608 | tf_op jit(solution)/shard_map/all_to_all | solution.py:108
  1147.2 22.8 %all-gather.35.cloned.1.call-done = bf16[1024,2,512]{0,2,1:T(8,128)(2,1)} async-done(((bf16[128,2,512]{0,2,1:T(8,128)(2,1)}), bf16[1024,2,512]{0,2,1:T(8,128)(2,1)}) %all-gather.35.cloned.1.call-update) | async-done | bytes 2097168 | tf_op jit(solution)/shard_map/all_gather | solution.py:112
  1170.0 2.9 multiply_convert_fusion
  1172.9 2.0 copy.30
  (68 shorter events, 20.0 us)
Async XLA Ops:
  7.2 28.3 %all-gather.13.cloned.1.call-start = ((), (), s32[]{:S(2)}) async-start(), calls=%async_computation.2 | async-start | bytes 2621440 | tf_op jit(solution)/shard_map/all_gather | solution.py:21
  9.2 0.8 copy-start.1
  10.0 315.7 %reduce-scatter.2.cloned.1.call-start = ((), (), s32[]{:S(2)}) async-start(), calls=%async_computation.3 | async-start | bytes 18874368 | tf_op jit(solution)/shard_map/reduce_scatter | solution.py:25
  45.3 337.1 %all-gather.15.cloned.1.call-start = ((), (), s32[]{:S(2)}) async-start(), calls=%async_computation.4 | async-start | bytes 1081344 | tf_op jit(solution)/shard_map/all_gather | solution.py:14
  325.7 58.3 %copy-start = (f32[256,4,512]{0,2,1:T(8,128)S(1)}, f32[256,4,512]{0,2,1:T(8,128)}, u32[]{:S(2)}) copy-start(f32[256,4,512]{0,2,1:T(8,128)} %reduce-scatter.2.cloned.1.call-done) | copy-start | bytes 6291460
  328.7 0.6 copy-start.4
  329.4 109.5 %all-gather.17.cloned.1.call-start = ((), (), s32[]{:S(2)}) async-start(), calls=%async_computation.5 | async-start | bytes 1081344 | tf_op jit(solution)/shard_map/all_gather | solution.py:14
  385.3 0.6 copy-start.5
  386.0 109.4 %all-gather.19.cloned.1.call-start = ((), (), s32[]{:S(2)}) async-start(), calls=%async_computation.6 | async-start | bytes 1081344 | tf_op jit(solution)/shard_map/all_gather | solution.py:14
  441.8 0.6 copy-start.3
  442.5 89.9 %all-gather.25.cloned.1.call-start = ((), (), s32[]{:S(2)}) async-start(), calls=%async_computation.9 | async-start | bytes 5242880 | tf_op jit(solution)/shard_map/all_gather | solution.py:21
  498.8 161.2 %all-gather.23.cloned.1.call-start = ((), (), s32[]{:S(2)}) async-start(), calls=%async_computation.8 | async-start | bytes 9437184 | tf_op jit(solution)/shard_map/all_gather | solution.py:34
  499.5 285.6 %all-gather.21.cloned.1.call-start = ((), (), s32[]{:S(2)}) async-start(), calls=%async_computation.7 | async-start | bytes 9437184 | tf_op jit(solution)/shard_map/all_gather | solution.py:34
  500.3 319.7 %all-gather.27.cloned.1.call-start = ((), (), s32[]{:S(2)}) async-start(), calls=%async_computation.10 | async-start | bytes 5242880 | tf_op jit(solution)/shard_map/all_gather | solution.py:21
  667.9 285.1 %all-gather.29.cloned.1.call-start = ((), (), s32[]{:S(2)}) async-start(), calls=%async_computation.11 | async-start | bytes 9437184 | tf_op jit(solution)/shard_map/all_gather | solution.py:34
  827.9 256.4 %all-gather.31.cloned.1.call-start = ((), (), s32[]{:S(2)}) async-start(), calls=%async_computation.12 | async-start | bytes 9437184 | tf_op jit(solution)/shard_map/all_gather | solution.py:34
  953.0 131.3 %copy-start.2 = (bf16[128,4,2048]{2,0,1:T(8,128)(2,1)S(1)}, bf16[128,4,2048]{2,0,1:T(8,128)(2,1)}, u32[]{:S(2)}) copy-start(bf16[128,4,2048]{2,0,1:T(8,128)(2,1)} %all-gather.13.cloned.1.call-done) | copy-start | bytes 6291460
  961.0 144.9 %all-gather.33.cloned.1.call-start = ((), (), s32[]{:S(2)}) async-start(), calls=%async_computation.13 | async-start | bytes 1310720 | tf_op jit(solution)/shard_map/all_gather | solution.py:21
  1090.9 79.1 %all-gather.35.cloned.1.call-start = ((), (), s32[]{:S(2)}) async-start(), calls=%async_computation.14 | async-start | bytes 2359296 | tf_op jit(solution)/shard_map/all_gather | solution.py:112
  1105.9 40.1 %all-to-all-start = ((bf16[128,8,512]{0,2,1:T(8,128)(2,1)}), bf16[128,8,512]{0,2,1:T(8,128)(2,1)S(1)}, u32[]{:S(2)}, u32[]{:S(2)}) async-start(bf16[128,8,512]{0,2,1:T(8,128)(2,1)} %bitcast.60), calls=%async_computation.1 | async-start | bytes 2097152 | tf_op jit(solution)/shard_map/all_to_all | solution.py:108
Sparse Core Ops, SparseCore 0:
  10.1 25.2 all-gather.12
  45.4 280.1 reduce-scatter.1
  329.5 52.8 all-gather.14
  386.1 52.7 all-gather.16
  442.6 52.7 all-gather.18
  498.9 33.4 all-gather.24
  535.0 124.9 all-gather.22
  662.0 123.1 all-gather.20
  787.3 32.6 all-gather.26
  828.0 124.9 all-gather.28
  961.1 123.1 all-gather.30
  1091.0 14.8 all-gather.32
  1108.5 61.4 all-gather.34
